TPU v7x, 32 devices: a whole 2x2x4 slice. The times are simulated.
32 devices in a mesh: dp: 8 (over z, x), mp: 4 (over y, core).
Axes of the slice: x: 2, y: 2, z: 4, core: 2. Of those that a mesh axis runs over, the one named last changes fastest.
Arguments:
- teacher_states: bfloat16 [512, 128, 4096], P('dp', None, 'mp'), may hold values from -6 to 6
- teacher_gain: float32 [4096], P('mp'), may hold values from 0.25 to 1.75
- teacher_proj: bfloat16 [4096, 1024], P('mp'), may hold values from -0.09375 to 0.09375
- teacher_mask: int32 [512, 128], P('dp'), may hold values 0 or 1
- student_states: bfloat16 [1024, 64, 768], P(('dp', 'mp')), may hold values from -6 to 6
- student_gain: float32 [768], replicated, may hold values from 0.25 to 1.75
- student_proj: bfloat16 [768, 1024], replicated, may hold values from -0.21875 to 0.21875
- student_mask: int32 [1024, 64], P(('dp', 'mp')), may hold values 0 or 1
- positive: int32 [1024], P(('dp', 'mp')), may hold values from 0 to 511
Outputs:
- grad_embed: float32 [1024, 1024], P(('dp', 'mp'))
- grad_states: bfloat16 [1024, 64, 768], P(('dp', 'mp'))
All inputs are finite; a program needn't handle non-finite values. No bound on the sum of `teacher_mask` or of `student_mask` on one device may be relied on, other than what follows from the above.
Results may differ from a plain program's by a relative error of at most 0.0085.
Values may be sent and summed in bfloat16 or wider, within the bound.
A program may use at most 128 MiB of HBM per device.

v0:
```python
import functools

import jax
import jax.numpy as jnp
from jax import lax
from jax.experimental import pallas as pl
from jax.experimental.pallas import tpu as pltpu
from jax.sharding import PartitionSpec as P

MESH = pl.DeviceIdType.MESH
F32 = jnp.float32
BF16 = jnp.bfloat16
GROUPS = 4
QC = 4
ROOT = 0.7978845608028654
CUBE = 0.044715
NT = (((1,), (1,)), ((), ()))


def spread(live, chunk, tokens):
    queries, length = live.shape
    wide = jnp.concatenate([live] * (tokens // length), axis=1)
    row = lax.broadcasted_iota(jnp.int32, (queries, tokens), 0)
    col = lax.broadcasted_iota(jnp.int32, (queries, tokens), 1)
    return jnp.where(row == chunk * (tokens // length) + col // length, wide, 0.0)


def front(
    dn, n, ts, tmask, tgain, tproj, ss, sgain, sproj, smask, pos,
    embed_out, grad_out, h_out,
    tx, tp, sx, sp, sq, sqr, tpool, pf, pb, pr, te, hbuf, raw_out,
    sem_tx, sem_in, sq_send, sq_recv, rs_send, rs_recv, ag_send, ag_recv, dp_send, dp_recv, fw_send, fw_recv, h_sem,
):
    passages, length, feats = tx.shape
    width = n * feats
    rows = passages // n
    embed = tp.shape[1]
    chunks = passages // 8
    tokens = QC * smask.shape[1]
    schunks = sx.shape[0] // tokens
    me_d, me_m = lax.axis_index("dp"), lax.axis_index("mp")

    def mp_peer(o):
        return (me_d, lax.rem(me_m + o, n))

    def dp_peer(o):
        return (lax.rem(me_d + o, dn), me_m)

    def load(c):
        part = pl.ds(c * 8, 8)
        return pltpu.make_async_copy(ts.at[part], tx.at[part], sem_tx.at[c])

    others = [
        pltpu.make_async_copy(ss, sx, sem_in.at[0]),
        pltpu.make_async_copy(sproj, sp, sem_in.at[1]),
        pltpu.make_async_copy(tproj, tp, sem_in.at[2]),
    ]
    ahead = min(4, chunks)
    for c in range(ahead):
        load(c).start()
    barrier = pltpu.get_barrier_semaphore()
    for o in range(1, n):
        pl.semaphore_signal(barrier, inc=1, device_id=mp_peer(o), device_id_type=MESH)
    for o in range(1, dn):
        pl.semaphore_signal(barrier, inc=1, device_id=dp_peer(o), device_id_type=MESH)

    def remote(src, dst, send, recv, peer):
        return pltpu.make_async_remote_copy(
            src_ref=src, dst_ref=dst, send_sem=send, recv_sem=recv, device_id=peer, device_id_type=MESH
        )

    ones = jnp.ones((16, 128), BF16)
    row8 = lax.broadcasted_iota(jnp.int32, (8, length), 0)
    per = chunks // GROUPS
    sq_copies = []
    for g in range(GROUPS):

        def squares(i, carry):
            c = g * per + i
            load(c).wait()

            @pl.when(c + ahead < chunks)
            def _():
                load(c + ahead).start()

            held = jnp.zeros((8, length), F32)
            for j in range(8):
                total = None
                for k in range(feats // 128):
                    x = tx[c * 8 + j, :, k * 128 : (k + 1) * 128].astype(F32)
                    total = x * x if total is None else total + x * x
                line = lax.dot_general(ones, total.astype(BF16), NT, preferred_element_type=F32)
                held = jnp.where(row8 == j, line[:8], held)
            sq[c] = held
            return carry

        lax.fori_loop(0, per, squares, 0)
        if g == 0:
            pl.semaphore_wait(barrier, n + dn - 2)
        if g == GROUPS // 2:
            for copy in others:
                copy.start()
        part = pl.ds(g * per, per)
        for o in range(1, n):
            copy = remote(sq.at[part], sqr.at[o, part], sq_send.at[o, g], sq_recv.at[o, g], mp_peer(o))
            copy.start()
            sq_copies.append(copy)

    row16 = lax.rem(lax.broadcasted_iota(jnp.int32, (16, length), 0), 8)
    for g in range(GROUPS):
        for o in range(1, n):
            sq_copies[g * (n - 1) + o - 1].wait_recv()

        def pool(i, carry):
            c = g * per + i
            total = sq[c]
            for o in range(1, n):
                total = total + sqr[o, c]
            part = pl.ds(pl.multiple_of(c * 8, 8), 8)
            weight = tmask[part, :].astype(F32) * lax.rsqrt(total / width + 1e-06)
            high = weight.astype(BF16).astype(F32)
            both = jnp.concatenate([high, weight - high], axis=0)
            left = jnp.concatenate([jnp.where(row16 == j, both, 0.0) for j in range(8)], axis=1).astype(BF16)
            sums = jnp.dot(left, tx[pl.ds(c * 8, 8)].reshape(8 * length, feats), preferred_element_type=F32)
            tpool[part, :] = (sums[:8] + sums[8:]) * tgain[...].reshape(1, feats)
            return carry

        lax.fori_loop(0, per, pool, 0)

    others[2].wait()
    partial = jnp.dot(tpool[...].astype(BF16), tp[...], preferred_element_type=F32)
    for j in range(n):
        block = partial[j * rows : (j + 1) * rows]
        pf[j] = block
        pb[j] = block.astype(BF16)
    rs_copies = []
    for o in range(1, n):
        copy = remote(pb.at[lax.rem(me_m + o, n)], pr.at[o], rs_send.at[o], rs_recv.at[o], mp_peer(o))
        copy.start()
        rs_copies.append(copy)

    live = smask[...].astype(F32)
    raw_out[...] = jnp.zeros_like(raw_out)
    others[0].wait()
    others[1].wait()

    def keep(i):
        part = pl.ds(pl.multiple_of(i * tokens, tokens), tokens)
        return pltpu.make_async_copy(hbuf.at[part], h_out.at[part], h_sem.at[i])

    def student(i, carry):
        part = pl.ds(pl.multiple_of(i * tokens, tokens), tokens)
        x = sx[part, :].astype(F32)
        scale = lax.rsqrt(jnp.mean(x * x, axis=-1, keepdims=True) + 1e-06)
        normed = (x * scale * sgain[...].reshape(1, sx.shape[1])).astype(BF16)
        picks = spread(live, i, tokens).astype(BF16)
        for k in range(embed // 256):
            cols = slice(k * 256, (k + 1) * 256)
            u = jnp.dot(normed, sp[:, cols], preferred_element_type=F32)
            uu = u * u
            th = jnp.tanh(u * (ROOT + (ROOT * CUBE) * uu))
            half = 0.5 + 0.5 * th
            act = u * half
            slope = half + act * (1.0 - th) * (ROOT + (3.0 * ROOT * CUBE) * uu)
            hbuf[part, cols] = slope.astype(BF16)
            raw_out[:, cols] += jnp.dot(picks, act.astype(BF16), preferred_element_type=F32)
        keep(i).start()
        return carry

    first, second, third = schunks // 4, 3 * schunks // 8, 7 * schunks // 8
    lax.fori_loop(0, first, student, 0)

    for copy in rs_copies:
        copy.wait_recv()
    summed = pf[me_m]
    for o in range(1, n):
        summed = summed + pr[o].astype(F32)
    unit = summed * lax.rsqrt(jnp.mean(summed * summed, axis=-1, keepdims=True) + 1e-06) * (embed ** -0.5)
    te[me_d, me_m] = unit.astype(BF16)
    ag_copies = []
    for o in range(1, n):
        copy = remote(te.at[me_d, me_m], te.at[me_d, me_m], ag_send.at[o], ag_recv.at[o], mp_peer(o))
        copy.start()
        ag_copies.append(copy)

    lax.fori_loop(first, second, student, 0)

    for copy in ag_copies:
        copy.wait_recv()
    dp_copies = []
    half = n // 2
    core = lax.rem(me_m, 2)
    mine = pl.ds(core * half, half)
    partner = (me_d, me_m + 1 - 2 * core)
    for o in range(1, dn):
        copy = remote(te.at[me_d, mine], te.at[me_d, mine], dp_send.at[o], dp_recv.at[o], dp_peer(o))
        copy.start()
        dp_copies.append(copy)

    lax.fori_loop(second, third, student, 0)

    fw_copies = []
    for o in range(1, dn):
        dp_copies[o - 1].wait_recv()
        came = te.at[lax.rem(me_d + dn - o, dn), mine]
        copy = remote(came, came, fw_send.at[o], fw_recv.at[o], partner)
        copy.start()
        fw_copies.append(copy)

    lax.fori_loop(third, schunks, student, 0)

    raw = raw_out[...]
    queries = raw.shape[0]
    scale = lax.rsqrt(jnp.mean(raw * raw, axis=-1, keepdims=True) + 1e-06)
    unit = scale * (embed ** -0.5)
    sround = (raw * unit).astype(BF16)
    total = dn * passages
    lines = lax.broadcasted_iota(jnp.int32, (total, queries), 0)
    picker = jnp.transpose(jnp.where(pos[...].reshape(1, queries) == lines, 1.0, 0.0)).astype(BF16)

    for copy in fw_copies:
        copy.wait_recv()
    table = te[...].reshape(total, embed)
    tpos = jnp.dot(picker, table, preferred_element_type=F32).astype(BF16)
    both = jnp.concatenate([tpos, sround], axis=0)
    logits = lax.dot_general(both, table, NT, preferred_element_type=F32)
    texp = jnp.exp(10.0 * logits[:queries])
    sexp = jnp.exp(20.0 * logits[queries:])
    diff = sexp / jnp.sum(sexp, axis=1, keepdims=True) - texp / jnp.sum(texp, axis=1, keepdims=True)
    ge = 20.0 * jnp.dot(diff.astype(BF16), table, preferred_element_type=F32)
    embed_out[...] = ge
    inner = jnp.mean(raw * ge, axis=-1, keepdims=True)
    grad_out[...] = unit * (ge - raw * (scale * scale * inner))
    for copy in sq_copies + rs_copies + ag_copies + dp_copies + fw_copies:
        copy.wait_send()
    for i in range(schunks):
        keep(i).wait()


def back(ge, grad, smask, sgain, sproj, ss, h, embed_out, states_out):
    step = pl.program_id(0)
    tokens = ss.shape[0]

    @pl.when(step == 0)
    def _():
        embed_out[...] = ge[...]

    picks = jnp.transpose(spread(smask[...].astype(F32), step, tokens)).astype(BF16)
    wide = jnp.dot(picks, grad[...].astype(BF16), preferred_element_type=F32)
    du = (h[...].astype(F32) * wide).astype(BF16)
    dn = lax.dot_general(du, sproj[...], NT, preferred_element_type=F32)
    gy = dn.astype(BF16).astype(F32) * sgain[...].reshape(1, ss.shape[1])
    x = ss[...].astype(F32)
    scale = lax.rsqrt(jnp.mean(x * x, axis=-1, keepdims=True) + 1e-06)
    inner = jnp.mean(x * gy, axis=-1, keepdims=True)
    states_out[...] = (scale * gy - x * (scale * scale * scale * inner)).astype(BF16)


def shards(dn, n, ts, tgain, tproj, tmask, ss, sgain, sproj, smask, positive):
    passages, length, feats = ts.shape
    embed = tproj.shape[1]
    queries, qlen, ds = ss.shape
    rows = passages // n
    total = queries * qlen
    tokens = QC * qlen
    schunks = total // tokens
    chunks = passages // 8
    flat = ss.reshape(total, ds)
    anyspace = pl.BlockSpec(memory_space=pl.ANY)
    vmem = pl.BlockSpec(memory_space=pltpu.VMEM)
    dma = pltpu.SemaphoreType.DMA
    ge, grad, h = pl.pallas_call(
        functools.partial(front, dn, n),
        out_shape=(
            jax.ShapeDtypeStruct((queries, embed), F32),
            jax.ShapeDtypeStruct((queries, embed), F32),
            jax.ShapeDtypeStruct((total, embed), BF16),
        ),
        in_specs=[anyspace, vmem, vmem, anyspace, anyspace, vmem, anyspace, vmem, vmem],
        out_specs=(vmem, vmem, anyspace),
        scratch_shapes=[
            pltpu.VMEM((passages, length, feats), BF16),
            pltpu.VMEM((feats, embed), BF16),
            pltpu.VMEM((total, ds), BF16),
            pltpu.VMEM((ds, embed), BF16),
            pltpu.VMEM((chunks, 8, length), F32),
            pltpu.VMEM((n, chunks, 8, length), F32),
            pltpu.VMEM((passages, feats), F32),
            pltpu.VMEM((n, rows, embed), F32),
            pltpu.VMEM((n, rows, embed), BF16),
            pltpu.VMEM((n, rows, embed), BF16),
            pltpu.VMEM((dn, n, rows, embed), BF16),
            pltpu.VMEM((total, embed), BF16),
            pltpu.VMEM((queries, embed), F32),
            dma((chunks,)),
            dma((3,)),
            dma((n, GROUPS)),
            dma((n, GROUPS)),
            dma((n,)),
            dma((n,)),
            dma((n,)),
            dma((n,)),
            dma((dn,)),
            dma((dn,)),
            dma((dn,)),
            dma((dn,)),
            dma((schunks,)),
        ],
        compiler_params=pltpu.CompilerParams(
            collective_id=0, has_side_effects=True, vmem_limit_bytes=56 * 1024 * 1024
        ),
        name="front",
    )(ts, tmask, tgain, tproj, flat, sgain, sproj, smask, positive)
    fixed = lambda shape: pl.BlockSpec(shape, lambda i: (0,) * len(shape))
    grad_embed, grad_states = pl.pallas_call(
        back,
        grid=(schunks,),
        out_shape=(jax.ShapeDtypeStruct((queries, embed), F32), jax.ShapeDtypeStruct((total, ds), BF16)),
        in_specs=[
            fixed((queries, embed)),
            fixed((queries, embed)),
            fixed((queries, qlen)),
            fixed((ds,)),
            fixed((ds, embed)),
            pl.BlockSpec((tokens, ds), lambda i: (i, 0)),
            pl.BlockSpec((tokens, embed), lambda i: (i, 0)),
        ],
        out_specs=(fixed((queries, embed)), pl.BlockSpec((tokens, ds), lambda i: (i, 0))),
        compiler_params=pltpu.CompilerParams(vmem_limit_bytes=62 * 1024 * 1024),
        name="back",
    )(ge, grad, smask, sgain, sproj, flat, h)
    return grad_embed, grad_states.reshape(queries, qlen, ds)


def solution(mesh):
    in_specs = (
        P("dp", None, "mp"),
        P("mp"),
        P("mp", None),
        P("dp", None),
        P(("dp", "mp"), None, None),
        P(),
        P(),
        P(("dp", "mp"), None),
        P(("dp", "mp")),
    )
    out_specs = (P(("dp", "mp"), None), P(("dp", "mp"), None, None))
    body = functools.partial(shards, mesh.shape["dp"], mesh.shape["mp"])
    return jax.shard_map(body, mesh=mesh, in_specs=in_specs, out_specs=out_specs, check_vma=False)
```

profile of v0, /device:TPU:8, one launch (start us, length us, event | category | flops | bytes accessed | tf_op | source)
XLA Modules:
  0.0 49.5 jit_solution(1773787105313959876)
XLA Ops:
  0.6 36.9 %front.1 = (f32[32,1024]{1,0:T(8,128)}, f32[32,1024]{1,0:T(8,128)}, bf16[2048,1024]{1,0:T(8,128)(2,1)}) custom-call(bf16[64,128,1024]{2,1,0:T(8,128)(2,1)} %ts.1, s32[64,128]{1,0:T(8,128)} %tmask.1, f32[1024]{0:T(1024)} %tgain.1, bf16[1024,1024]{1,0:T(8,128)(2,1)} %tproj.1, bf16[2048,768]{1,0:T(8,128)(2,1)} %bitcast.2, f32[768]{0:T(1024)} %sgain.3, ...), custom_call_target="tpu_custom_call" | custom-call | tf_op jit(solution)/shard_map/front/pallas_call | solution.py:272
  37.6 12.0 %back.1 = (f32[32,1024]{1,0:T(8,128)}, bf16[2048,768]{1,0:T(8,128)(2,1)}) custom-call(f32[32,1024]{1,0:T(8,128)} %get-tuple-element.7.ge, f32[32,1024]{1,0:T(8,128)} %get-tuple-element.8.grad, s32[32,64]{1,0:T(8,128)} %smask.3, f32[768]{0:T(1024)} %sgain.3, bf16[768,1024]{1,0:T(8,128)(2,1)} %sproj.3, bf16[2048,768]{1,0:T(8,128)(2,1)} %bitcast.3, ...), custom_call_target="tpu_custom_call" | custom-call | tf_op jit(solution)/shard_map/back/pallas_call | solution.py:315
where the time goes:
time: 49.9 us; the launch traced here: 49.5 us
  Pallas kernels  48.9 us (98%)
  between operations  0.64 us (1%)
    pallas_call x1, Pallas kernels, shards(): pl.pallas_call(functools.partial(front, dn, n), out_shape=(jax.ShapeDtype...  36.9 us
    pallas_call x1, Pallas kernels, shards(): pl.pallas_call(back, grid=(schunks,), out_shape=(jax.ShapeDtypeStruct((qu...  12 us

commit v1 on v0

v1 whole, which is shorter than its diff:
```python
import functools

import jax
import jax.numpy as jnp
from jax import lax
from jax.experimental import pallas as pl
from jax.experimental.pallas import tpu as pltpu
from jax.sharding import PartitionSpec as P

MESH = pl.DeviceIdType.MESH
F32 = jnp.float32
BF16 = jnp.bfloat16
GROUPS = 4
ROOT = 0.7978845608028654
CUBE = 0.044715
LANES = 128
TILE = 256
NT = (((1,), (1,)), ((), ()))


def nearest(count):
    order = []
    for step in range(1, count // 2 + 1):
        order.append(step)
        if count - step != step:
            order.append(count - step)
    return order


def front(
    dn, n, ts, tmask, tgain, tproj, ss, sgain, sproj, smask, pos,
    ge_out, grad_out, h_out, x_out, scl_out, wt_out,
    tx, tp, sp, sw, live_col, sq, sqr, tpool, pf, pb, pr, te, raw_out, ua, ub,
    sem_tx, sem_in, sq_send, sq_recv, rs_send, rs_recv, dp_send, dp_recv, col_send, col_recv, fw_send, fw_recv,
):
    passages, length, feats = tx.shape
    width = n * feats
    rows = passages // n
    embed = tp.shape[1]
    chunks = passages // 8
    queries, qlen = smask.shape
    ds = sp.shape[0]
    tokens = TILE
    per_tile = tokens // qlen
    bodies = queries // (2 * per_tile)
    me_d, me_m = lax.axis_index("dp"), lax.axis_index("mp")
    half = n // 2
    core, chip = lax.rem(me_m, 2), me_m // 2

    def mp_peer(o):
        return (me_d, lax.rem(me_m + o, n))

    def dp_peer(o):
        return (lax.rem(me_d + o, dn), me_m)

    def col_peer(p):
        return (me_d, 2 * lax.rem(chip + p, half) + core)

    partner = (me_d, me_m + 1 - 2 * core)

    def load(c):
        part = pl.ds(c * 8, 8)
        return pltpu.make_async_copy(ts.at[part], tx.at[part], sem_tx.at[c])

    others = [
        pltpu.make_async_copy(sproj, sp, sem_in.at[0]),
        pltpu.make_async_copy(tproj, tp, sem_in.at[1]),
        pltpu.make_async_copy(ss, x_out, sem_in.at[2]),
    ]
    ahead = min(4, chunks)
    for c in range(ahead):
        load(c).start()
    barrier = pltpu.get_barrier_semaphore()
    for o in range(1, n):
        pl.semaphore_signal(barrier, inc=1, device_id=mp_peer(o), device_id_type=MESH)
    for o in range(1, dn):
        pl.semaphore_signal(barrier, inc=1, device_id=dp_peer(o), device_id_type=MESH)

    def remote(src, dst, send, recv, peer):
        return pltpu.make_async_remote_copy(
            src_ref=src, dst_ref=dst, send_sem=send, recv_sem=recv, device_id=peer, device_id_type=MESH
        )

    turned = jnp.transpose(smask[...].astype(F32))
    for q in range(queries):
        live_col[q * qlen : (q + 1) * qlen, :] = jnp.broadcast_to(turned[:, q : q + 1], (qlen, LANES))

    ones = jnp.ones((16, LANES), BF16)
    row8 = lax.broadcasted_iota(jnp.int32, (8, length), 0)
    row16 = lax.rem(lax.broadcasted_iota(jnp.int32, (16, length), 0), 8)
    per = chunks // GROUPS
    sq_copies = []

    def squares(c, carry):
        load(c).wait()

        @pl.when(c + ahead < chunks)
        def _():
            load(c + ahead).start()

        held = jnp.zeros((8, length), F32)
        for j in range(8):
            terms = []
            for k in range(feats // LANES):
                x = tx[c * 8 + j, :, k * LANES : (k + 1) * LANES]
                terms.append(x * x)
            while len(terms) > 1:
                terms = [a + b for a, b in zip(terms[::2], terms[1::2])] + terms[len(terms) // 2 * 2 :]
            line = lax.dot_general(ones, terms[0], NT, preferred_element_type=F32)
            held = jnp.where(row8 == j, line[:8], held)
        sq[c] = held
        return carry

    def send_squares(g):
        part = pl.ds(g * per, per)
        for o in range(1, n):
            copy = remote(sq.at[part], sqr.at[o, part], sq_send.at[o, g], sq_recv.at[o, g], mp_peer(o))
            copy.start()
            sq_copies.append(copy)

    def pool(c, carry):
        total = sq[c]
        for o in range(1, n):
            total = total + sqr[o, c]
        part = pl.ds(pl.multiple_of(c * 8, 8), 8)
        weight = tmask[part, :].astype(F32) * lax.rsqrt(total / width + 1e-06)
        high = weight.astype(BF16).astype(F32)
        both = jnp.concatenate([high, weight - high], axis=0)
        left = jnp.concatenate([jnp.where(row16 == j, both, 0.0) for j in range(8)], axis=1).astype(BF16)
        sums = jnp.dot(left, tx[pl.ds(c * 8, 8)].reshape(8 * length, feats), preferred_element_type=F32)
        tpool[part, :] = (sums[:8] + sums[8:]) * tgain[...].reshape(1, feats)
        return carry

    def pooling(g):
        for o in range(1, n):
            sq_copies[g * (n - 1) + o - 1].wait_recv()
        lax.fori_loop(g * per, (g + 1) * per, pool, 0)

    lax.fori_loop(0, 2 * per, squares, 0)
    pl.semaphore_wait(barrier, n + dn - 2)
    for copy in others:
        copy.start()
    send_squares(0)
    send_squares(1)
    lax.fori_loop(2 * per, 3 * per, squares, 0)
    send_squares(2)
    lax.fori_loop(3 * per, 4 * per, squares, 0)
    send_squares(3)
    pooling(0)
    pooling(1)
    pooling(2)

    others[0].wait()
    gain_col = jnp.transpose(jnp.broadcast_to(sgain[...].reshape(1, ds), (LANES, ds)))

    def weigh(k, carry):
        cols = pl.ds(pl.multiple_of(k * LANES, LANES), LANES)
        scaled = (sp[:, cols].astype(F32) * gain_col).astype(BF16)
        sw[:, cols] = scaled
        wt_out[cols, :] = jnp.transpose(scaled)
        return carry

    lax.fori_loop(0, embed // LANES, weigh, 0)
    pooling(3)

    others[1].wait()
    partial = jnp.dot(tpool[...].astype(BF16), tp[...], preferred_element_type=F32)
    for j in range(n):
        block = partial[j * rows : (j + 1) * rows]
        pf[j] = block
        pb[j] = block.astype(BF16)
    rs_copies = []
    for o in range(1, n):
        copy = remote(pb.at[lax.rem(me_m + o, n)], pr.at[o], rs_send.at[o], rs_recv.at[o], mp_peer(o))
        copy.start()
        rs_copies.append(copy)

    others[2].wait()
    tiles = embed // TILE
    stages = (ua, ub)

    def chunk(c):
        return pl.ds(pl.multiple_of(c * tokens, tokens), tokens)

    def multiply(c, k, out):
        out[...] = jnp.dot(x_out[chunk(c), :], sw[:, k * TILE : (k + 1) * TILE], preferred_element_type=F32)

    def rescale(c):
        x = x_out[chunk(c), :].astype(F32)
        scale = lax.rsqrt(jnp.mean(x * x, axis=-1, keepdims=True) + 1e-06)
        scl_out[chunk(c), :] = live_col[chunk(c), :] * scale

    group8 = lax.broadcasted_iota(jnp.int32, (2 * per_tile, tokens), 0)
    token8 = lax.broadcasted_iota(jnp.int32, (2 * per_tile, tokens), 1) // qlen
    picks = [jnp.where(group8 == token8 + s * per_tile, 1.0, 0.0).astype(BF16) for s in range(2)]

    def activate(c, i, side, k, held):
        cols = slice(k * TILE, (k + 1) * TILE)
        scale = scl_out[chunk(c), :]
        u = held[...] * jnp.concatenate([scale] * (TILE // LANES), axis=1)
        z = (u * (ROOT + (ROOT * CUBE) * (u * u))).astype(BF16)
        ul = u.astype(BF16)
        th = jnp.tanh(z)
        part = th * BF16(0.5) + BF16(0.5)
        act = ul * part
        bend = (ul * ul) * BF16(3.0 * ROOT * CUBE) + BF16(ROOT)
        h_out[chunk(c), cols] = part + act * (BF16(1.0) - th) * bend
        summed = jnp.dot(picks[side], act, preferred_element_type=F32)
        spot = pl.ds(pl.multiple_of(i * 2 * per_tile, 2 * per_tile), 2 * per_tile)
        if side == 0:
            raw_out[spot, cols] = summed
        else:
            raw_out[spot, cols] += summed

    def student(i, carry):
        here = (2 * i, 2 * i + 1)
        after = jnp.minimum(2 * i + 2, 2 * bodies - 1)
        for side in range(2):
            for k in range(tiles):
                step = side * tiles + k
                if k + 1 < tiles:
                    multiply(here[side], k + 1, stages[(step + 1) % 2])
                else:
                    multiply(here[1] if side == 0 else after, 0, stages[(step + 1) % 2])
                if k == 0:
                    rescale(here[1] if side == 0 else after)
                activate(here[side], i, side, k, stages[step % 2])
        return carry

    rescale(0)
    multiply(0, 0, stages[0])
    first, second, third = bodies // 2, 3 * bodies // 4, bodies
    lax.fori_loop(0, first, student, 0)

    for copy in rs_copies:
        copy.wait_recv()
    summed = pf[me_m]
    for o in range(1, n):
        summed = summed + pr[o].astype(F32)
    unit = summed * lax.rsqrt(jnp.mean(summed * summed, axis=-1, keepdims=True) + 1e-06) * (embed ** -0.5)
    te[me_d, core, chip] = unit.astype(BF16)
    order = nearest(dn)
    dp_copies, col_copies, fw_copies = {}, {}, {}
    for o in order:
        own = te.at[me_d, core, chip]
        dp_copies[o] = remote(own, own, dp_send.at[o], dp_recv.at[o], dp_peer(o))
        dp_copies[o].start()

    def share(o):
        block = te.at[lax.rem(me_d + dn - o, dn), core, chip]
        for p in range(1, half):
            col_copies[o, p] = remote(block, block, col_send.at[o, p], col_recv.at[o, p], col_peer(p))
            col_copies[o, p].start()

    def pass_on(o):
        for p in range(1, half):
            col_copies[o, p].wait_recv()
        block = te.at[lax.rem(me_d + dn - o, dn), core]
        fw_copies[o] = remote(block, block, fw_send.at[o], fw_recv.at[o], partner)
        fw_copies[o].start()

    share(0)
    lax.fori_loop(first, second, student, 0)
    for o in order[: len(order) // 2]:
        dp_copies[o].wait_recv()
        share(o)
    pass_on(0)
    lax.fori_loop(second, third, student, 0)
    for o in order[len(order) // 2 :]:
        dp_copies[o].wait_recv()
        share(o)

    raw = raw_out[...]
    scale = lax.rsqrt(jnp.mean(raw * raw, axis=-1, keepdims=True) + 1e-06)
    unit = scale * (embed ** -0.5)
    sround = (raw * unit).astype(BF16)
    total = dn * passages
    place = lax.broadcasted_iota(jnp.int32, (total, queries), 0)
    block, row = place // rows, lax.rem(place, rows)
    owner, slot = block // n, lax.rem(block, n)
    lines = (owner * n + lax.rem(slot, half) * 2 + slot // half) * rows + row
    picker = jnp.transpose(jnp.where(pos[...].reshape(1, queries) == lines, 1.0, 0.0)).astype(BF16)

    for o in order:
        pass_on(o)
    for o in [0] + order:
        fw_copies[o].wait_recv()
    table = te[...].reshape(total, embed)
    tpos = jnp.dot(picker, table, preferred_element_type=F32).astype(BF16)
    both = jnp.concatenate([tpos, sround], axis=0)
    logits = lax.dot_general(both, table, NT, preferred_element_type=F32)
    texp = jnp.exp(10.0 * logits[:queries])
    sexp = jnp.exp(20.0 * logits[queries:])
    diff = sexp / jnp.sum(sexp, axis=1, keepdims=True) - texp / jnp.sum(texp, axis=1, keepdims=True)
    ge = 20.0 * jnp.dot(diff.astype(BF16), table, preferred_element_type=F32)
    ge_out[...] = ge
    inner = jnp.mean(raw * ge, axis=-1, keepdims=True)
    grad_out[...] = unit * (ge - raw * (scale * scale * inner))
    for copy in sq_copies + rs_copies + list(dp_copies.values()) + list(col_copies.values()) + list(fw_copies.values()):
        copy.wait_send()


def back(ge, grad, h, xs, scl, wt, embed_out, states_out, ga, gb, staged, embed_sem, sem):
    total, embed = h.shape
    ds = xs.shape[1]
    queries = grad.shape[0]
    qlen = total // queries
    tokens = TILE
    count = total // tokens
    per_tile = tokens // qlen
    keep = pltpu.make_async_copy(ge, embed_out, embed_sem)
    keep.start()

    def chunk(c):
        return pl.ds(pl.multiple_of(c * tokens, tokens), tokens)

    def store(c):
        return pltpu.make_async_copy(staged.at[chunk(c)], states_out.at[chunk(c)], sem.at[c])

    def multiply(c, out):
        pieces = []
        for j in range(per_tile):
            line = jnp.broadcast_to(grad[pl.ds(c * per_tile + j, 1), :], (16, embed)).astype(BF16)
            part = pl.ds(pl.multiple_of(c * tokens + j * qlen, qlen), qlen)
            pieces.append(h[part, :] * jnp.concatenate([line] * (qlen // 16), axis=0))
        out[...] = jnp.dot(jnp.concatenate(pieces, axis=0), wt[...], preferred_element_type=F32)

    def finish(c, held):
        gy = held[...]
        x = xs[chunk(c), :].astype(F32)
        scale = scl[chunk(c), :]
        inner = jnp.mean(x * gy, axis=-1, keepdims=True)
        bias = scale * scale * inner
        wide = lambda v: jnp.concatenate([v] * (ds // LANES), axis=1)
        staged[chunk(c), :] = (wide(scale) * (gy - x * wide(bias))).astype(BF16)
        store(c).start()

    multiply(0, ga)

    def body(i, carry):
        multiply(2 * i + 1, gb)
        finish(2 * i, ga)
        multiply(2 * i + 2, ga)
        finish(2 * i + 1, gb)
        return carry

    lax.fori_loop(0, count // 2 - 1, body, 0)
    multiply(count - 1, gb)
    finish(count - 2, ga)
    finish(count - 1, gb)
    keep.wait()
    for c in range(count):
        store(c).wait()


def shards(dn, n, ts, tgain, tproj, tmask, ss, sgain, sproj, smask, positive):
    passages, length, feats = ts.shape
    embed = tproj.shape[1]
    queries, qlen, ds = ss.shape
    rows = passages // n
    total = queries * qlen
    chunks = passages // 8
    flat = ss.reshape(total, ds)
    hbm = pl.BlockSpec(memory_space=pltpu.HBM)
    vmem = pl.BlockSpec(memory_space=pltpu.VMEM)
    dma = pltpu.SemaphoreType.DMA
    ge, grad, h, xs, scl, wt = pl.pallas_call(
        functools.partial(front, dn, n),
        out_shape=(
            pltpu.VMEM((queries, embed), F32),
            pltpu.VMEM((queries, embed), F32),
            pltpu.VMEM((total, embed), BF16),
            pltpu.VMEM((total, ds), BF16),
            pltpu.VMEM((total, LANES), F32),
            pltpu.VMEM((embed, ds), BF16),
        ),
        in_specs=[hbm, vmem, vmem, hbm, hbm, vmem, hbm, vmem, vmem],
        out_specs=(vmem,) * 6,
        scratch_shapes=[
            pltpu.VMEM((passages, length, feats), BF16),
            pltpu.VMEM((feats, embed), BF16),
            pltpu.VMEM((ds, embed), BF16),
            pltpu.VMEM((ds, embed), BF16),
            pltpu.VMEM((total, LANES), F32),
            pltpu.VMEM((chunks, 8, length), F32),
            pltpu.VMEM((n, chunks, 8, length), F32),
            pltpu.VMEM((passages, feats), F32),
            pltpu.VMEM((n, rows, embed), F32),
            pltpu.VMEM((n, rows, embed), BF16),
            pltpu.VMEM((n, rows, embed), BF16),
            pltpu.VMEM((dn, 2, n // 2, rows, embed), BF16),
            pltpu.VMEM((queries, embed), F32),
            pltpu.VMEM((TILE, TILE), F32),
            pltpu.VMEM((TILE, TILE), F32),
            dma((chunks,)),
            dma((3,)),
            dma((n, GROUPS)),
            dma((n, GROUPS)),
            dma((n,)),
            dma((n,)),
            dma((dn,)),
            dma((dn,)),
            dma((dn, n // 2)),
            dma((dn, n // 2)),
            dma((dn,)),
            dma((dn,)),
        ],
        compiler_params=pltpu.CompilerParams(
            collective_id=0, has_side_effects=True, vmem_limit_bytes=56_600_000
        ),
        name="front",
    )(ts, tmask, tgain, tproj, flat, sgain, sproj, smask, positive)
    grad_embed, grad_states = pl.pallas_call(
        back,
        out_shape=(jax.ShapeDtypeStruct((queries, embed), F32), jax.ShapeDtypeStruct((total, ds), BF16)),
        in_specs=[vmem] * 6,
        out_specs=(hbm, hbm),
        scratch_shapes=[
            pltpu.VMEM((TILE, ds), F32),
            pltpu.VMEM((TILE, ds), F32),
            pltpu.VMEM((total, ds), BF16),
            dma,
            dma((total // TILE,)),
        ],
        compiler_params=pltpu.CompilerParams(vmem_limit_bytes=16 * 1024 * 1024),
        name="back",
    )(ge, grad, h, xs, scl, wt)
    return grad_embed, grad_states.reshape(queries, qlen, ds)


def solution(mesh):
    in_specs = (
        P("dp", None, "mp"),
        P("mp"),
        P("mp", None),
        P("dp", None),
        P(("dp", "mp"), None, None),
        P(),
        P(),
        P(("dp", "mp"), None),
        P(("dp", "mp")),
    )
    out_specs = (P(("dp", "mp"), None), P(("dp", "mp"), None, None))
    body = functools.partial(shards, mesh.shape["dp"], mesh.shape["mp"])
    return jax.shard_map(body, mesh=mesh, in_specs=in_specs, out_specs=out_specs, check_vma=False)
```

time: 49.9 us -> 41 us (0.82)
  the two profiles are of different devices: /device:TPU:8 before, /device:TPU:1 now
where the time goes in v1:
time: 41 us; the launch traced here: 40.8 us
  Pallas kernels  40.1 us (98%)
  between operations  0.64 us (2%)
    pallas_call x1, Pallas kernels, shards(): pl.pallas_call(functools.partial(front, dn, n), out_shape=(pltpu.VMEM((qu...  34.4 us
    pallas_call x1, Pallas kernels, shards(): pl.pallas_call(back, out_shape=(jax.ShapeDtypeStruct((queries, embed), F3...  5.69 us

profile of v1, /device:TPU:1, one launch (start us, length us, event | category | flops | bytes accessed | tf_op | source)
XLA Modules:
  0.0 40.8 jit_solution(17047645012212165966)
XLA Ops:
  0.6 34.4 %front.1 = (f32[32,1024]{1,0:T(8,128)S(1)}, f32[32,1024]{1,0:T(8,128)S(1)}, bf16[2048,1024]{1,0:T(8,128)(2,1)S(1)}, bf16[2048,768]{1,0:T(8,128)(2,1)S(1)}, f32[2...) custom-call(bf16[64,128,1024]{2,1,0:T(8,128)(2,1)} %ts.1, s32[64,128]{1,0:T(8,128)} %tmask.1, f32[1024]{0:T(1024)} %tgain.1, ...), custom_call_target="tpu_custom_call" | custom-call | tf_op jit(solution)/shard_map/front/pallas_call | solution.py:367
  35.1 5.7 %back.1 = (f32[32,1024]{1,0:T(8,128)}, bf16[2048,768]{1,0:T(8,128)(2,1)}) custom-call(f32[32,1024]{1,0:T(8,128)S(1)} %get-tuple-element.10.ge, f32[32,1024]{1,0:T(8,128)S(1)} %get-tuple-element.11.grad, bf16[2048,1024]{1,0:T(8,128)(2,1)S(1)} %get-tuple-element.12.h, bf16[2048,768]{1,0:T(8,128)(2,1)S(1)} %get-tuple-element.13.xs, ...), custom_call_target="tpu_custom_call" | custom-call | tf_op jit(solution)/shard_map/back/pallas_call | solution.py:413

commit v2 on v1

v2 whole, which is shorter than its diff:
```python
import functools

import jax
import jax.numpy as jnp
from jax import lax
from jax.experimental import pallas as pl
from jax.experimental.pallas import tpu as pltpu
from jax.sharding import PartitionSpec as P

MESH = pl.DeviceIdType.MESH
F32 = jnp.float32
BF16 = jnp.bfloat16
GROUPS = 4
AHEAD = 5
ROOT = 0.7978845608028654
CUBE = 0.044715
LANES = 128
TILE = 256
SLAB = 16
NT = (((1,), (1,)), ((), ()))


def nearest(count):
    return [sorted(range(count), key=lambda other: abs(other - here))[1:] for here in range(count)]


def choose(index, values):
    picked = values[0]
    for i, value in enumerate(values[1:], 1):
        picked = jnp.where(index == i, value, picked)
    return picked


def front(
    dn, n, ts, tmask, tgain, tproj, ss, sgain, sproj, smask, pos,
    ge_out, grad_out, h_out, x_out, scl_out, wt_out,
    tx, tp, sp, sw, tm, tg, sg, sm, po, live_col, sq, sqr, tpool, pf, pb, pr, te, raw_out, ua, ub, aa, ab, ca, cb,
    sem_tx, sem_in, sq_send, sq_recv, rs_send, rs_recv, z_send, z_recv, plane_send, plane_recv, fw_send, fw_recv,
):
    passages, length, feats = tx.shape
    width = n * feats
    rows = passages // n
    embed = tp.shape[1]
    chunks = passages // 8
    queries, qlen = sm.shape
    ds = sp.shape[0]
    tokens = TILE
    per_tile = tokens // qlen
    me_d, me_m = lax.axis_index("dp"), lax.axis_index("mp")
    half = n // 2
    core, chip = lax.rem(me_m, 2), me_m // 2

    def mp_peer(o):
        return (me_d, lax.rem(me_m + o, n))

    def dp_peer(o):
        return (lax.rem(me_d + o, dn), me_m)

    side_x = 2 if dn % 2 == 0 else 1
    depth = dn // side_x
    me_z, me_x = me_d // side_x, lax.rem(me_d, side_x)

    def plane_peer(p):
        x = lax.rem(me_x + p // half, side_x)
        return (me_z * side_x + x, 2 * lax.rem(chip + p % half, half) + core)

    partner = (me_d, me_m + 1 - 2 * core)

    def load(c):
        part = pl.ds(c * 8, 8)
        return pltpu.make_async_copy(ts.at[part], tx.at[part], sem_tx.at[lax.rem(c, ahead)])

    ahead = min(AHEAD, chunks)
    moves = [(smask, sm), (tmask, tm), (tgain, tg), (sgain, sg), (pos, po), (tproj, tp), (sproj, sp), (ss, x_out)]
    copies = [pltpu.make_async_copy(a, b, sem_in.at[i]) for i, (a, b) in enumerate(moves)]
    small, others = copies[:5], copies[5:]
    for copy in small:
        copy.start()
    for c in range(ahead):
        load(c).start()
    barrier = pltpu.get_barrier_semaphore()
    for o in range(1, n):
        pl.semaphore_signal(barrier, inc=1, device_id=mp_peer(o), device_id_type=MESH)
    for o in range(1, dn):
        pl.semaphore_signal(barrier, inc=1, device_id=dp_peer(o), device_id_type=MESH)

    def remote(src, dst, send, recv, peer):
        return pltpu.make_async_remote_copy(
            src_ref=src, dst_ref=dst, send_sem=send, recv_sem=recv, device_id=peer, device_id_type=MESH
        )

    def spread_mask():
        for copy in small:
            copy.wait()
        turned = jnp.transpose(sm[...].astype(F32))
        for q in range(queries):
            live_col[q * qlen : (q + 1) * qlen, :] = jnp.broadcast_to(turned[:, q : q + 1], (qlen, LANES))

    ones = jnp.ones((16, TILE), BF16)
    row8 = lax.broadcasted_iota(jnp.int32, (8, length), 0)
    row16 = lax.rem(lax.broadcasted_iota(jnp.int32, (16, length), 0), 8)
    per = chunks // GROUPS

    def squares(c, carry):
        load(c).wait()

        @pl.when(c + ahead < chunks)
        def _():
            load(c + ahead).start()

        held = jnp.zeros((8, length), F32)
        for j in range(8):
            terms = []
            for k in range(feats // TILE):
                x = tx[c * 8 + j, :, k * TILE : (k + 1) * TILE]
                terms.append(x * x)
            while len(terms) > 1:
                terms = [a + b for a, b in zip(terms[::2], terms[1::2])] + terms[len(terms) // 2 * 2 :]
            line = lax.dot_general(ones, terms[0], NT, preferred_element_type=F32)
            held = jnp.where(row8 == j, line[:8], held)
        sq[c] = held
        return carry

    def send_squares(g):
        part = pl.ds(g * per, per)
        for o in range(1, n):
            remote(sq.at[part], sqr.at[g, o - 1], sq_send, sq_recv.at[g], mp_peer(o)).start()

    def pool(g, i, carry):
        c = g * per + i
        total = sq[c]
        for o in range(1, n):
            total = total + sqr[g, o - 1, i]
        part = pl.ds(pl.multiple_of(c * 8, 8), 8)
        weight = tm[part, :].astype(F32) * lax.rsqrt(total / width + 1e-06)
        high = weight.astype(BF16).astype(F32)
        both = jnp.concatenate([high, weight - high], axis=0)
        left = jnp.concatenate([jnp.where(row16 == j, both, 0.0) for j in range(8)], axis=1).astype(BF16)
        sums = jnp.dot(left, tx[pl.ds(c * 8, 8)].reshape(8 * length, feats), preferred_element_type=F32)
        tpool[part, :] = (sums[:8] + sums[8:]) * tg[...].reshape(1, feats)
        return carry

    def pooling(g):
        remote(sqr.at[g], sqr.at[g], sq_send, sq_recv.at[g], partner).wait_recv()
        lax.fori_loop(0, per, functools.partial(pool, g), 0)

    lax.fori_loop(0, per, squares, 0)
    pl.semaphore_wait(barrier, n + dn - 2)
    send_squares(0)
    lax.fori_loop(per, 2 * per, squares, 0)
    for copy in others:
        copy.start()
    send_squares(1)
    spread_mask()
    lax.fori_loop(2 * per, 3 * per, squares, 0)
    send_squares(2)
    lax.fori_loop(3 * per, 4 * per, squares, 0)
    send_squares(3)
    for g in range(GROUPS):
        pooling(g)

    others[0].wait()
    partial = jnp.dot(tpool[...].astype(BF16), tp[...], preferred_element_type=F32)
    for j in range(n):
        block = partial[j * rows : (j + 1) * rows]
        pf[j] = block
        pb[j] = block.astype(BF16)
    for o in range(1, n):
        remote(pb.at[lax.rem(me_m + o, n)], pr.at[o - 1], rs_send, rs_recv, mp_peer(o)).start()

    others[1].wait()
    gain_col = jnp.transpose(jnp.broadcast_to(sg[...].reshape(1, ds), (LANES, ds)))

    def weigh(k, carry):
        cols = pl.ds(pl.multiple_of(k * LANES, LANES), LANES)
        scaled = (sp[:, cols].astype(F32) * gain_col).astype(BF16)
        sw[k] = scaled
        for j in range(ds // LANES):
            wt_out[j, cols, :] = jnp.transpose(scaled[j * LANES : (j + 1) * LANES])
        return carry

    lax.fori_loop(0, embed // LANES, weigh, 0)
    others[2].wait()
    stages = ((ua, aa, ca), (ub, ab, cb))
    count = queries // per_tile

    def chunk(c):
        return pl.ds(pl.multiple_of(c * tokens, tokens), tokens)

    tiles = embed // TILE

    def prepare(c, side, k):
        out, _, scale_out = stages[side]
        right = jnp.concatenate([sw[k * (TILE // LANES) + j] for j in range(TILE // LANES)], axis=1)
        out[:, k * TILE : (k + 1) * TILE] = jnp.dot(x_out[chunk(c), :], right, preferred_element_type=F32)

    def rescale(c, side, k):
        scale_out = stages[side][2]
        for r in range(k * tokens // tiles, (k + 1) * tokens // tiles, SLAB):
            part = pl.ds(pl.multiple_of(c * tokens + r, SLAB), SLAB)
            x = x_out[part, :].astype(F32)
            scale = live_col[part, :] * lax.rsqrt(jnp.mean(x * x, axis=-1, keepdims=True) + 1e-06)
            scale_out[r : r + SLAB, :] = scale
            scl_out[part, :] = scale

    group8 = lax.broadcasted_iota(jnp.int32, (2 * per_tile, tokens), 0)
    token8 = lax.broadcasted_iota(jnp.int32, (2 * per_tile, tokens), 1) // qlen
    picks = [jnp.where(group8 == token8 + side * per_tile, 1.0, 0.0).astype(BF16) for side in range(2)]

    def activate(c, side, k):
        held, kept, scale_in = stages[side]
        cols = slice(k * TILE, (k + 1) * TILE)
        for r in range(0, tokens, SLAB):
            u = held[r : r + SLAB, cols] * jnp.concatenate([scale_in[r : r + SLAB, :]] * (TILE // LANES), axis=1)
            z = (u * (ROOT + (ROOT * CUBE) * (u * u))).astype(BF16)
            ul = u.astype(BF16)
            th = jnp.tanh(z)
            part = th * BF16(0.5) + BF16(0.5)
            act = ul * part
            bend = (ul * ul) * BF16(3.0 * ROOT * CUBE) + BF16(ROOT)
            kept[r : r + SLAB, cols] = act
            spot = pl.ds(pl.multiple_of(c * tokens + r, SLAB), SLAB)
            h_out[spot, cols] = part + act * (BF16(1.0) - th) * bend

    def total_up(c, side, k):
        cols = slice(k * TILE, (k + 1) * TILE)
        summed = jnp.dot(picks[side], stages[side][1][:, cols], preferred_element_type=F32)
        spot = pl.ds(pl.multiple_of(c // 2 * (2 * per_tile), 2 * per_tile), 2 * per_tile)
        if side == 0:
            raw_out[spot, cols] = summed
        else:
            raw_out[spot, cols] += summed

    def student(c, carry):
        for side in range(2):

            @pl.when(lax.rem(c, 2) == side)
            def _():
                for k in range(tiles):
                    total_up(jnp.maximum(c - 1, 0), 1 - side, k)
                    rescale(jnp.minimum(c + 1, count - 1), 1 - side, k)
                for k in range(tiles):
                    prepare(jnp.minimum(c + 1, count - 1), 1 - side, k)
                    activate(c, side, k)

        return carry

    ab[...] = jnp.zeros_like(ab)
    raw_out[...] = jnp.zeros_like(raw_out)
    for k in range(tiles):
        prepare(0, 0, k)
        rescale(0, 0, k)
    marks = [count * j // 8 for j in (0, 2, 4, 5, 6, 7, 8)]

    def work(stage):
        lax.fori_loop(marks[stage], marks[stage + 1], student, 0)

    work(0)
    remote(pr, pr, rs_send, rs_recv, partner).wait_recv()
    summed = pf[me_m]
    for o in range(1, n):
        summed = summed + pr[o - 1].astype(F32)
    unit = summed * lax.rsqrt(jnp.mean(summed * summed, axis=-1, keepdims=True) + 1e-06) * (embed ** -0.5)
    te[me_z, core, me_x, chip] = unit.astype(BF16)
    order = nearest(depth)
    peers = side_x * half - 1
    own = te.at[me_z, core, me_x, chip]
    gathered = te.reshape(depth * 2 * side_x * half, rows, embed).at[pl.ds(0, peers)]

    def near(j):
        return choose(me_z, [order[z][j] for z in range(depth)])

    for j in range(depth - 1):
        z = near(depth - 2 - j)
        remote(own, own, z_send, z_recv.at[me_z], (z * side_x + me_x, me_m)).start()

    def share(z):
        block = te.at[z, core, me_x, chip]
        for p in range(peers, 0, -1):
            remote(block, block, plane_send, plane_recv.at[z], plane_peer(p)).start()

    def pass_on(z):
        if peers:
            remote(gathered, gathered, plane_send, plane_recv.at[z], partner).wait_recv()
        block = te.at[z, core]
        remote(block, block, fw_send, fw_recv.at[z], partner).start()

    def relay(j):
        z = near(j)
        block = te.at[z, core, me_x, chip]
        remote(block, block, z_send, z_recv.at[z], partner).wait_recv()
        share(z)

    share(me_z)
    work(1)
    for j in range(depth - 1):
        relay(j)
        if j < 3:
            work(2 + j)
        if j == 1:
            pass_on(me_z)
    for j in range(min(3, depth - 1), 4):
        work(2 + j)
    for k in range(tiles):
        total_up(count - 1, 1, k)
    for j in range(depth - 2):
        pass_on(near(j))

    raw = raw_out[...]
    scale = lax.rsqrt(jnp.mean(raw * raw, axis=-1, keepdims=True) + 1e-06)
    unit = scale * (embed ** -0.5)
    sround = (raw * unit).astype(BF16)
    total = dn * passages
    place = lax.broadcasted_iota(jnp.int32, (total, queries), 0)
    block, row = place // rows, lax.rem(place, rows)
    plane, slot = block // (side_x * n), lax.rem(block, side_x * n)
    owner = plane * side_x + lax.rem(slot // half, side_x)
    member = lax.rem(slot, half) * 2 + slot // (half * side_x)
    lines = (owner * n + member) * rows + row
    picker = jnp.transpose(jnp.where(po[...].reshape(1, queries) == lines, 1.0, 0.0)).astype(BF16)

    pass_on(near(depth - 2))
    for j in range(depth):
        span = te.at[me_z, core]
        remote(span, span, fw_send, fw_recv.at[j], partner).wait_recv()
    table = te[...].reshape(total, embed)
    tpos = jnp.dot(picker, table, preferred_element_type=F32).astype(BF16)
    both = jnp.concatenate([tpos, sround], axis=0)
    logits = lax.dot_general(both, table, NT, preferred_element_type=F32)
    texp = jnp.exp(10.0 * logits[:queries])
    sexp = jnp.exp(20.0 * logits[queries:])
    diff = sexp / jnp.sum(sexp, axis=1, keepdims=True) - texp / jnp.sum(texp, axis=1, keepdims=True)
    ge = 20.0 * jnp.dot(diff.astype(BF16), table, preferred_element_type=F32)
    ge_out[...] = ge
    inner = jnp.mean(raw * ge, axis=-1, keepdims=True)
    grad_out[...] = unit * (ge - raw * (scale * scale * inner))
    remote(sqr, sqr, sq_send, sq_recv.at[0], partner).wait_send()
    remote(pr, pr, rs_send, rs_recv, partner).wait_send()
    sent = te.at[pl.ds(0, depth - 1), 0, 0, 0]
    remote(sent, sent, z_send, z_recv.at[0], partner).wait_send()
    if peers:
        for z in range(depth):
            remote(gathered, gathered, plane_send, plane_recv.at[0], partner).wait_send()
    sent = te.at[:, 0]
    remote(sent, sent, fw_send, fw_recv.at[0], partner).wait_send()


def back(ge, grad, h, xs, scl, wt, embed_out, states_out, ga, gb, staged, embed_sem, sem):
    total, embed = h.shape
    ds = xs.shape[1]
    queries = grad.shape[0]
    qlen = total // queries
    tokens = TILE
    count = total // tokens
    per_tile = tokens // qlen
    keep = pltpu.make_async_copy(ge, embed_out, embed_sem)
    keep.start()

    def chunk(c):
        return pl.ds(pl.multiple_of(c * tokens, tokens), tokens)

    def store(c):
        return pltpu.make_async_copy(staged.at[chunk(c)], states_out.at[chunk(c)], sem.at[c])

    def multiply(c, out):
        pieces = []
        for j in range(per_tile):
            line = jnp.broadcast_to(grad[pl.ds(c * per_tile + j, 1), :], (16, embed)).astype(BF16)
            part = pl.ds(pl.multiple_of(c * tokens + j * qlen, qlen), qlen)
            pieces.append(h[part, :] * jnp.concatenate([line] * (qlen // 16), axis=0))
        left = jnp.concatenate(pieces, axis=0)
        for k in range(ds // TILE):
            right = jnp.concatenate([wt[k * (TILE // LANES) + j] for j in range(TILE // LANES)], axis=1)
            out[:, k * TILE : (k + 1) * TILE] = jnp.dot(left, right, preferred_element_type=F32)

    def finish(c, held):
        gy = held[...]
        x = xs[chunk(c), :].astype(F32)
        scale = scl[chunk(c), :]
        inner = jnp.mean(x * gy, axis=-1, keepdims=True)
        bias = scale * scale * inner
        wide = lambda v: jnp.concatenate([v] * (ds // LANES), axis=1)
        staged[chunk(c), :] = (wide(scale) * (gy - x * wide(bias))).astype(BF16)
        store(c).start()

    multiply(0, ga)

    def body(i, carry):
        multiply(2 * i + 1, gb)
        finish(2 * i, ga)
        multiply(2 * i + 2, ga)
        finish(2 * i + 1, gb)
        return carry

    lax.fori_loop(0, count // 2 - 1, body, 0)
    multiply(count - 1, gb)
    finish(count - 2, ga)
    finish(count - 1, gb)
    keep.wait()
    for c in range(count):
        store(c).wait()


def shards(dn, n, ts, tgain, tproj, tmask, ss, sgain, sproj, smask, positive):
    passages, length, feats = ts.shape
    embed = tproj.shape[1]
    queries, qlen, ds = ss.shape
    rows = passages // n
    total = queries * qlen
    chunks = passages // 8
    side_x = 2 if dn % 2 == 0 else 1
    flat = ss.reshape(total, ds)
    hbm = pl.BlockSpec(memory_space=pltpu.HBM)
    vmem = pl.BlockSpec(memory_space=pltpu.VMEM)
    dma = pltpu.SemaphoreType.DMA
    ge, grad, h, xs, scl, wt = pl.pallas_call(
        functools.partial(front, dn, n),
        out_shape=(
            pltpu.VMEM((queries, embed), F32),
            pltpu.VMEM((queries, embed), F32),
            pltpu.VMEM((total, embed), BF16),
            pltpu.VMEM((total, ds), BF16),
            pltpu.VMEM((total, LANES), F32),
            pltpu.VMEM((ds // LANES, embed, LANES), BF16),
        ),
        in_specs=[hbm] * 9,
        out_specs=(vmem,) * 6,
        scratch_shapes=[
            pltpu.VMEM((passages, length, feats), BF16),
            pltpu.VMEM((feats, embed), BF16),
            pltpu.VMEM((ds, embed), BF16),
            pltpu.VMEM((embed // LANES, ds, LANES), BF16),
            pltpu.VMEM((passages, length), jnp.int32),
            pltpu.VMEM((feats,), F32),
            pltpu.VMEM((ds,), F32),
            pltpu.VMEM((queries, qlen), jnp.int32),
            pltpu.VMEM((queries,), jnp.int32),
            pltpu.VMEM((total, LANES), F32),
            pltpu.VMEM((chunks, 8, length), F32),
            pltpu.VMEM((GROUPS, n - 1, chunks // GROUPS, 8, length), F32),
            pltpu.VMEM((passages, feats), F32),
            pltpu.VMEM((n, rows, embed), F32),
            pltpu.VMEM((n, rows, embed), BF16),
            pltpu.VMEM((n - 1, rows, embed), BF16),
            pltpu.VMEM((dn // side_x, 2, side_x, n // 2, rows, embed), BF16),
            pltpu.VMEM((queries, embed), F32),
            pltpu.VMEM((TILE, embed), F32),
            pltpu.VMEM((TILE, embed), F32),
            pltpu.VMEM((TILE, embed), BF16),
            pltpu.VMEM((TILE, embed), BF16),
            pltpu.VMEM((TILE, LANES), F32),
            pltpu.VMEM((TILE, LANES), F32),
            dma((min(AHEAD, chunks),)),
            dma((8,)),
            dma,
            dma((GROUPS,)),
            dma,
            dma,
            dma,
            dma((dn // side_x,)),
            dma,
            dma((dn // side_x,)),
            dma,
            dma((dn // side_x,)),
        ],
        compiler_params=pltpu.CompilerParams(
            collective_id=0, has_side_effects=True, vmem_limit_bytes=56_600_000
        ),
        name="front",
    )(ts, tmask, tgain, tproj, flat, sgain, sproj, smask, positive)
    grad_embed, grad_states = pl.pallas_call(
        back,
        out_shape=(jax.ShapeDtypeStruct((queries, embed), F32), jax.ShapeDtypeStruct((total, ds), BF16)),
        in_specs=[vmem] * 6,
        out_specs=(hbm, hbm),
        scratch_shapes=[
            pltpu.VMEM((TILE, ds), F32),
            pltpu.VMEM((TILE, ds), F32),
            pltpu.VMEM((total, ds), BF16),
            dma,
            dma((total // TILE,)),
        ],
        compiler_params=pltpu.CompilerParams(vmem_limit_bytes=16 * 1024 * 1024),
        name="back",
    )(ge, grad, h, xs, scl, wt)
    return grad_embed, grad_states.reshape(queries, qlen, ds)


def solution(mesh):
    in_specs = (
        P("dp", None, "mp"),
        P("mp"),
        P("mp", None),
        P("dp", None),
        P(("dp", "mp"), None, None),
        P(),
        P(),
        P(("dp", "mp"), None),
        P(("dp", "mp")),
    )
    out_specs = (P(("dp", "mp"), None), P(("dp", "mp"), None, None))
    body = functools.partial(shards, mesh.shape["dp"], mesh.shape["mp"])
    return jax.shard_map(body, mesh=mesh, in_specs=in_specs, out_specs=out_specs, check_vma=False)
```

time: 41 us -> 34.3 us (0.84)
  Pallas kernels: 40.1 us -> 33.5 us
    pallas_call x1, Pallas kernels: 34.4 us -> 27.9 us  [shards(): pl.pallas_call(functools.partial(front, dn, n), out_shape=(pltpu.VMEM((qu...]
where the time goes in v2:
time: 34.3 us; the launch traced here: 34.2 us
  Pallas kernels  33.5 us (98%)
  between operations  0.64 us (2%)
    pallas_call x1, Pallas kernels, shards(): pl.pallas_call(functools.partial(front, dn, n), out_shape=(pltpu.VMEM((qu...  27.9 us
    pallas_call x1, Pallas kernels, shards(): pl.pallas_call(back, out_shape=(jax.ShapeDtypeStruct((queries, embed), F3...  5.64 us

profile of v2, /device:TPU:1, one launch (start us, length us, event | category | flops | bytes accessed | tf_op | source)
XLA Modules:
  0.0 34.2 jit_solution(9555722276410750684)
XLA Ops:
  0.6 27.9 %front.1 = (f32[32,1024]{1,0:T(8,128)S(1)}, f32[32,1024]{1,0:T(8,128)S(1)}, bf16[2048,1024]{1,0:T(8,128)(2,1)S(1)}, bf16[2048,768]{1,0:T(8,128)(2,1)S(1)}, f32[2...) custom-call(bf16[64,128,1024]{2,1,0:T(8,128)(2,1)} %ts.1, s32[64,128]{1,0:T(8,128)} %tmask.1, f32[1024]{0:T(1024)} %tgain.1, ...), custom_call_target="tpu_custom_call" | custom-call | tf_op jit(solution)/shard_map/front/pallas_call | solution.py:416
  28.5 5.6 %back.1 = (f32[32,1024]{1,0:T(8,128)}, bf16[2048,768]{1,0:T(8,128)(2,1)}) custom-call(f32[32,1024]{1,0:T(8,128)S(1)} %get-tuple-element.10.ge, f32[32,1024]{1,0:T(8,128)S(1)} %get-tuple-element.11.grad, bf16[2048,1024]{1,0:T(8,128)(2,1)S(1)} %get-tuple-element.12.h, bf16[2048,768]{1,0:T(8,128)(2,1)S(1)} %get-tuple-element.13.xs, ...), custom_call_target="tpu_custom_call" | custom-call | tf_op jit(solution)/shard_map/back/pallas_call | solution.py:471

commit v3 on v2

--- a/solution.py
+++ b/solution.py
@@ -24,6 +24,10 @@
     return [sorted(range(count), key=lambda other: abs(other - here))[1:] for here in range(count)]
 
 
+def halves_of(passages, n):
+    return 2 if passages // n % 16 == 0 else 1
+
+
 def choose(index, values):
     picked = values[0]
     for i, value in enumerate(values[1:], 1):
@@ -39,7 +43,9 @@
 ):
     passages, length, feats = tx.shape
     width = n * feats
-    rows = passages // n
+    parts = halves_of(passages, n)
+    rows = passages // (n * parts)
+    span = passages // parts
     embed = tp.shape[1]
     chunks = passages // 8
     queries, qlen = sm.shape
@@ -142,31 +148,73 @@
 
     def pooling(g):
         remote(sqr.at[g], sqr.at[g], sq_send, sq_recv.at[g], partner).wait_recv()
-        lax.fori_loop(0, per, functools.partial(pool, g), 0)
+        lax.fori_loop(0, per, functools.partial(pool, g), 0, unroll=True)
 
     lax.fori_loop(0, per, squares, 0)
     pl.semaphore_wait(barrier, n + dn - 2)
     send_squares(0)
     lax.fori_loop(per, 2 * per, squares, 0)
-    for copy in others:
-        copy.start()
     send_squares(1)
     spread_mask()
     lax.fori_loop(2 * per, 3 * per, squares, 0)
     send_squares(2)
     lax.fori_loop(3 * per, 4 * per, squares, 0)
     send_squares(3)
-    for g in range(GROUPS):
-        pooling(g)
-
-    others[0].wait()
-    partial = jnp.dot(tpool[...].astype(BF16), tp[...], preferred_element_type=F32)
-    for j in range(n):
-        block = partial[j * rows : (j + 1) * rows]
-        pf[j] = block
-        pb[j] = block.astype(BF16)
-    for o in range(1, n):
-        remote(pb.at[lax.rem(me_m + o, n)], pr.at[o - 1], rs_send, rs_recv, mp_peer(o)).start()
+    for copy in others:
+        copy.start()
+    def project(b):
+        partial = jnp.dot(tpool[b * span : (b + 1) * span, :].astype(BF16), tp[...], preferred_element_type=F32)
+        for j in range(n):
+            block = partial[j * rows : (j + 1) * rows]
+            pf[b, j] = block
+            pb[b, j] = block.astype(BF16)
+        for o in range(1, n):
+            remote(pb.at[b, lax.rem(me_m + o, n)], pr.at[b, o - 1], rs_send, rs_recv.at[b], mp_peer(o)).start()
+
+    for b in range(parts):
+        for g in range(b * GROUPS // parts, (b + 1) * GROUPS // parts):
+            pooling(g)
+        if b == 0:
+            others[0].wait()
+        project(b)
+
+    order = nearest(depth)
+    peers = side_x * half - 1
+    gathered = te.reshape(parts * depth * 2 * side_x * half, rows, embed).at[pl.ds(0, peers)]
+
+    def near(j):
+        return choose(me_z, [order[z][j] for z in range(depth)])
+
+    def share(b, z):
+        block = te.at[b, z, core, me_x, chip]
+        for p in range(peers, 0, -1):
+            remote(block, block, plane_send, plane_recv.at[b, z], plane_peer(p)).start()
+
+    def launch(b):
+        remote(pr.at[b], pr.at[b], rs_send, rs_recv.at[b], partner).wait_recv()
+        summed = pf[b, me_m]
+        for o in range(1, n):
+            summed = summed + pr[b, o - 1].astype(F32)
+        unit = summed * lax.rsqrt(jnp.mean(summed * summed, axis=-1, keepdims=True) + 1e-06) * (embed ** -0.5)
+        te[b, me_z, core, me_x, chip] = unit.astype(BF16)
+        own = te.at[b, me_z, core, me_x, chip]
+        for j in range(depth - 1):
+            z = near(depth - 2 - j)
+            remote(own, own, z_send, z_recv.at[b, me_z], (z * side_x + me_x, me_m)).start()
+        share(b, me_z)
+
+    def pass_on(b, z):
+        if peers:
+            remote(gathered, gathered, plane_send, plane_recv.at[b, z], partner).wait_recv()
+        block = te.at[b, z, core]
+        remote(block, block, fw_send, fw_recv.at[b, z], partner).start()
+
+    def relay(b):
+        for j in range(depth - 1):
+            z = near(j)
+            block = te.at[b, z, core, me_x, chip]
+            remote(block, block, z_send, z_recv.at[b, z], partner).wait_recv()
+            share(b, z)
 
     others[1].wait()
     gain_col = jnp.transpose(jnp.broadcast_to(sg[...].reshape(1, ds), (LANES, ds)))
@@ -180,6 +228,8 @@
         return carry
 
     lax.fori_loop(0, embed // LANES, weigh, 0)
+    if parts > 1:
+        launch(0)
     others[2].wait()
     stages = ((ua, aa, ca), (ub, ab, cb))
     count = queries // per_tile
@@ -250,61 +300,27 @@
     for k in range(tiles):
         prepare(0, 0, k)
         rescale(0, 0, k)
-    marks = [count * j // 8 for j in (0, 2, 4, 5, 6, 7, 8)]
+    marks = [count * j // 8 for j in (0, 1, 2, 4, 7, 8)]
 
     def work(stage):
         lax.fori_loop(marks[stage], marks[stage + 1], student, 0)
 
     work(0)
-    remote(pr, pr, rs_send, rs_recv, partner).wait_recv()
-    summed = pf[me_m]
-    for o in range(1, n):
-        summed = summed + pr[o - 1].astype(F32)
-    unit = summed * lax.rsqrt(jnp.mean(summed * summed, axis=-1, keepdims=True) + 1e-06) * (embed ** -0.5)
-    te[me_z, core, me_x, chip] = unit.astype(BF16)
-    order = nearest(depth)
-    peers = side_x * half - 1
-    own = te.at[me_z, core, me_x, chip]
-    gathered = te.reshape(depth * 2 * side_x * half, rows, embed).at[pl.ds(0, peers)]
-
-    def near(j):
-        return choose(me_z, [order[z][j] for z in range(depth)])
-
-    for j in range(depth - 1):
-        z = near(depth - 2 - j)
-        remote(own, own, z_send, z_recv.at[me_z], (z * side_x + me_x, me_m)).start()
-
-    def share(z):
-        block = te.at[z, core, me_x, chip]
-        for p in range(peers, 0, -1):
-            remote(block, block, plane_send, plane_recv.at[z], plane_peer(p)).start()
-
-    def pass_on(z):
-        if peers:
-            remote(gathered, gathered, plane_send, plane_recv.at[z], partner).wait_recv()
-        block = te.at[z, core]
-        remote(block, block, fw_send, fw_recv.at[z], partner).start()
-
-    def relay(j):
-        z = near(j)
-        block = te.at[z, core, me_x, chip]
-        remote(block, block, z_send, z_recv.at[z], partner).wait_recv()
-        share(z)
-
-    share(me_z)
+    launch(parts - 1)
     work(1)
-    for j in range(depth - 1):
-        relay(j)
-        if j < 3:
-            work(2 + j)
-        if j == 1:
-            pass_on(me_z)
-    for j in range(min(3, depth - 1), 4):
-        work(2 + j)
+    if parts > 1:
+        relay(0)
+    work(2)
+    relay(parts - 1)
+    if parts > 1:
+        pass_on(0, me_z)
+    work(3)
+    if parts > 1:
+        for j in range(depth - 1):
+            pass_on(0, near(j))
+    work(4)
     for k in range(tiles):
         total_up(count - 1, 1, k)
-    for j in range(depth - 2):
-        pass_on(near(j))
 
     raw = raw_out[...]
     scale = lax.rsqrt(jnp.mean(raw * raw, axis=-1, keepdims=True) + 1e-06)
@@ -313,16 +329,20 @@
     total = dn * passages
     place = lax.broadcasted_iota(jnp.int32, (total, queries), 0)
     block, row = place // rows, lax.rem(place, rows)
+    piece, block = block // (dn * n), lax.rem(block, dn * n)
     plane, slot = block // (side_x * n), lax.rem(block, side_x * n)
     owner = plane * side_x + lax.rem(slot // half, side_x)
     member = lax.rem(slot, half) * 2 + slot // (half * side_x)
-    lines = (owner * n + member) * rows + row
+    lines = owner * passages + piece * span + member * rows + row
     picker = jnp.transpose(jnp.where(po[...].reshape(1, queries) == lines, 1.0, 0.0)).astype(BF16)
 
-    pass_on(near(depth - 2))
-    for j in range(depth):
-        span = te.at[me_z, core]
-        remote(span, span, fw_send, fw_recv.at[j], partner).wait_recv()
+    pass_on(parts - 1, me_z)
+    for j in range(depth - 1):
+        pass_on(parts - 1, near(j))
+    for b in range(parts):
+        for z in range(depth):
+            column = te.at[b, z, core]
+            remote(column, column, fw_send, fw_recv.at[b, z], partner).wait_recv()
     table = te[...].reshape(total, embed)
     tpos = jnp.dot(picker, table, preferred_element_type=F32).astype(BF16)
     both = jnp.concatenate([tpos, sround], axis=0)
@@ -335,14 +355,14 @@
     inner = jnp.mean(raw * ge, axis=-1, keepdims=True)
     grad_out[...] = unit * (ge - raw * (scale * scale * inner))
     remote(sqr, sqr, sq_send, sq_recv.at[0], partner).wait_send()
-    remote(pr, pr, rs_send, rs_recv, partner).wait_send()
-    sent = te.at[pl.ds(0, depth - 1), 0, 0, 0]
-    remote(sent, sent, z_send, z_recv.at[0], partner).wait_send()
+    remote(pr, pr, rs_send, rs_recv.at[0], partner).wait_send()
+    sent = te.at[:, pl.ds(0, depth - 1), 0, 0, 0]
+    remote(sent, sent, z_send, z_recv.at[0, 0], partner).wait_send()
     if peers:
-        for z in range(depth):
-            remote(gathered, gathered, plane_send, plane_recv.at[0], partner).wait_send()
-    sent = te.at[:, 0]
-    remote(sent, sent, fw_send, fw_recv.at[0], partner).wait_send()
+        for j in range(parts * depth):
+            remote(gathered, gathered, plane_send, plane_recv.at[0, 0], partner).wait_send()
+    sent = te.at[:, :, 0]
+    remote(sent, sent, fw_send, fw_recv.at[0, 0], partner).wait_send()
 
 
 def back(ge, grad, h, xs, scl, wt, embed_out, states_out, ga, gb, staged, embed_sem, sem):
@@ -392,7 +412,7 @@
         finish(2 * i + 1, gb)
         return carry
 
-    lax.fori_loop(0, count // 2 - 1, body, 0)
+    lax.fori_loop(0, count // 2 - 1, body, 0, unroll=True)
     multiply(count - 1, gb)
     finish(count - 2, ga)
     finish(count - 1, gb)
@@ -405,7 +425,8 @@
     passages, length, feats = ts.shape
     embed = tproj.shape[1]
     queries, qlen, ds = ss.shape
-    rows = passages // n
+    parts = halves_of(passages, n)
+    rows = passages // (n * parts)
     total = queries * qlen
     chunks = passages // 8
     side_x = 2 if dn % 2 == 0 else 1
@@ -439,10 +460,10 @@
             pltpu.VMEM((chunks, 8, length), F32),
             pltpu.VMEM((GROUPS, n - 1, chunks // GROUPS, 8, length), F32),
             pltpu.VMEM((passages, feats), F32),
-            pltpu.VMEM((n, rows, embed), F32),
-            pltpu.VMEM((n, rows, embed), BF16),
-            pltpu.VMEM((n - 1, rows, embed), BF16),
-            pltpu.VMEM((dn // side_x, 2, side_x, n // 2, rows, embed), BF16),
+            pltpu.VMEM((parts, n, rows, embed), F32),
+            pltpu.VMEM((parts, n, rows, embed), BF16),
+            pltpu.VMEM((parts, n - 1, rows, embed), BF16),
+            pltpu.VMEM((parts, dn // side_x, 2, side_x, n // 2, rows, embed), BF16),
             pltpu.VMEM((queries, embed), F32),
             pltpu.VMEM((TILE, embed), F32),
             pltpu.VMEM((TILE, embed), F32),
@@ -455,13 +476,13 @@
             dma,
             dma((GROUPS,)),
             dma,
+            dma((parts,)),
             dma,
+            dma((parts, dn // side_x)),
             dma,
-            dma((dn // side_x,)),
+            dma((parts, dn // side_x)),
             dma,
-            dma((dn // side_x,)),
-            dma,
-            dma((dn // side_x,)),
+            dma((parts, dn // side_x)),
         ],
         compiler_params=pltpu.CompilerParams(
             collective_id=0, has_side_effects=True, vmem_limit_bytes=56_600_000

time: 34.3 us -> 32.9 us (0.959)
  Pallas kernels: 33.5 us -> 31.9 us
    pallas_call x1, Pallas kernels: 27.9 us -> 26.9 us  [shards(): pl.pallas_call(functools.partial(front, dn, n), out_shape=(pltpu.VMEM((qu...]
    pallas_call x1, Pallas kernels: 5.64 us -> 5.02 us  [shards(): pl.pallas_call(back, out_shape=(jax.ShapeDtypeStruct((queries, embed), F3...]
where the time goes in v3:
time: 32.9 us; the launch traced here: 32.7 us
  Pallas kernels  31.9 us (97%)
  between operations  0.8 us (2%)
    pallas_call x1, Pallas kernels, shards(): pl.pallas_call(functools.partial(front, dn, n), out_shape=(pltpu.VMEM((qu...  26.9 us
    pallas_call x1, Pallas kernels, shards(): pl.pallas_call(back, out_shape=(jax.ShapeDtypeStruct((queries, embed), F3...  5.02 us

profile of v3, /device:TPU:1, one launch (start us, length us, event | category | flops | bytes accessed | tf_op | source)
XLA Modules:
  0.0 32.7 jit_solution(8406665850039445081)
XLA Ops:
  0.6 26.9 %front.1 = (f32[32,1024]{1,0:T(8,128)S(1)}, f32[32,1024]{1,0:T(8,128)S(1)}, bf16[2048,1024]{1,0:T(8,128)(2,1)S(1)}, bf16[2048,768]{1,0:T(8,128)(2,1)S(1)}, f32[2...) custom-call(bf16[64,128,1024]{2,1,0:T(8,128)(2,1)} %ts.1, s32[64,128]{1,0:T(8,128)} %tmask.1, f32[1024]{0:T(1024)} %tgain.1, ...), custom_call_target="tpu_custom_call" | custom-call | tf_op jit(solution)/shard_map/front/pallas_call | solution.py:437
  27.5 5.0 %back.1 = (f32[32,1024]{1,0:T(8,128)}, bf16[2048,768]{1,0:T(8,128)(2,1)}) custom-call(f32[32,1024]{1,0:T(8,128)S(1)} %get-tuple-element.10.ge, f32[32,1024]{1,0:T(8,128)S(1)} %get-tuple-element.11.grad, bf16[2048,1024]{1,0:T(8,128)(2,1)S(1)} %get-tuple-element.12.h, bf16[2048,768]{1,0:T(8,128)(2,1)S(1)} %get-tuple-element.13.xs, ...), custom_call_target="tpu_custom_call" | custom-call | tf_op jit(solution)/shard_map/back/pallas_call | solution.py:492

commit v4 on v3

--- a/solution.py
+++ b/solution.py
@@ -38,7 +38,7 @@
 def front(
     dn, n, ts, tmask, tgain, tproj, ss, sgain, sproj, smask, pos,
     ge_out, grad_out, h_out, x_out, scl_out, wt_out,
-    tx, tp, sp, sw, tm, tg, sg, sm, po, live_col, sq, sqr, tpool, pf, pb, pr, te, raw_out, ua, ub, aa, ab, ca, cb,
+    tx, tp, sp, sw, tm, tg, sg, sm, po, live_col, sq, sqr, tpool, pf, pb, pr, te, wanted, raw_out, ua, ub, aa, ab, ca, cb,
     sem_tx, sem_in, sq_send, sq_recv, rs_send, rs_recv, z_send, z_recv, plane_send, plane_recv, fw_send, fw_recv,
 ):
     passages, length, feats = tx.shape
@@ -300,7 +300,7 @@
     for k in range(tiles):
         prepare(0, 0, k)
         rescale(0, 0, k)
-    marks = [count * j // 8 for j in (0, 1, 2, 4, 7, 8)]
+    marks = [count * j // 8 for j in (0, 1, 3, 4, 7, 8)]
 
     def work(stage):
         lax.fori_loop(marks[stage], marks[stage + 1], student, 0)
@@ -308,6 +308,15 @@
     work(0)
     launch(parts - 1)
     work(1)
+    total = dn * passages
+    place = lax.broadcasted_iota(jnp.int32, (total, queries), 0)
+    block, row = place // rows, lax.rem(place, rows)
+    piece, block = block // (dn * n), lax.rem(block, dn * n)
+    plane, slot = block // (side_x * n), lax.rem(block, side_x * n)
+    owner = plane * side_x + lax.rem(slot // half, side_x)
+    member = lax.rem(slot, half) * 2 + slot // (half * side_x)
+    lines = owner * passages + piece * span + member * rows + row
+    wanted[...] = jnp.transpose(jnp.where(po[...].reshape(1, queries) == lines, 1.0, 0.0)).astype(BF16)
     if parts > 1:
         relay(0)
     work(2)
@@ -318,7 +327,9 @@
     if parts > 1:
         for j in range(depth - 1):
             pass_on(0, near(j))
+    pass_on(parts - 1, me_z)
     work(4)
+    pass_on(parts - 1, near(0))
     for k in range(tiles):
         total_up(count - 1, 1, k)
 
@@ -326,25 +337,14 @@
     scale = lax.rsqrt(jnp.mean(raw * raw, axis=-1, keepdims=True) + 1e-06)
     unit = scale * (embed ** -0.5)
     sround = (raw * unit).astype(BF16)
-    total = dn * passages
-    place = lax.broadcasted_iota(jnp.int32, (total, queries), 0)
-    block, row = place // rows, lax.rem(place, rows)
-    piece, block = block // (dn * n), lax.rem(block, dn * n)
-    plane, slot = block // (side_x * n), lax.rem(block, side_x * n)
-    owner = plane * side_x + lax.rem(slot // half, side_x)
-    member = lax.rem(slot, half) * 2 + slot // (half * side_x)
-    lines = owner * passages + piece * span + member * rows + row
-    picker = jnp.transpose(jnp.where(po[...].reshape(1, queries) == lines, 1.0, 0.0)).astype(BF16)
-
-    pass_on(parts - 1, me_z)
-    for j in range(depth - 1):
+    for j in range(1, depth - 1):
         pass_on(parts - 1, near(j))
     for b in range(parts):
         for z in range(depth):
             column = te.at[b, z, core]
             remote(column, column, fw_send, fw_recv.at[b, z], partner).wait_recv()
     table = te[...].reshape(total, embed)
-    tpos = jnp.dot(picker, table, preferred_element_type=F32).astype(BF16)
+    tpos = jnp.dot(wanted[...], table, preferred_element_type=F32).astype(BF16)
     both = jnp.concatenate([tpos, sround], axis=0)
     logits = lax.dot_general(both, table, NT, preferred_element_type=F32)
     texp = jnp.exp(10.0 * logits[:queries])
@@ -464,6 +464,7 @@
             pltpu.VMEM((parts, n, rows, embed), BF16),
             pltpu.VMEM((parts, n - 1, rows, embed), BF16),
             pltpu.VMEM((parts, dn // side_x, 2, side_x, n // 2, rows, embed), BF16),
+            pltpu.VMEM((queries, dn * passages), BF16),
             pltpu.VMEM((queries, embed), F32),
             pltpu.VMEM((TILE, embed), F32),
             pltpu.VMEM((TILE, embed), F32),

time: 32.9 us -> 32.6 us (level)
  no operation moved by 1% of the time
where the time goes in v4:
time: 32.6 us; the launch traced here: 32.4 us
  Pallas kernels  31.6 us (97%)
  between operations  0.8 us (2%)
    pallas_call x1, Pallas kernels, shards(): pl.pallas_call(functools.partial(front, dn, n), out_shape=(pltpu.VMEM((qu...  26.6 us
    pallas_call x1, Pallas kernels, shards(): pl.pallas_call(back, out_shape=(jax.ShapeDtypeStruct((queries, embed), F3...  5.02 us

profile of v4, /device:TPU:1, one launch (start us, length us, event | category | flops | bytes accessed | tf_op | source)
XLA Modules:
  0.0 32.4 jit_solution(8181840339614307194)
XLA Ops:
  0.6 26.6 %front.1 = (f32[32,1024]{1,0:T(8,128)S(1)}, f32[32,1024]{1,0:T(8,128)S(1)}, bf16[2048,1024]{1,0:T(8,128)(2,1)S(1)}, bf16[2048,768]{1,0:T(8,128)(2,1)S(1)}, f32[2...) custom-call(bf16[64,128,1024]{2,1,0:T(8,128)(2,1)} %ts.1, s32[64,128]{1,0:T(8,128)} %tmask.1, f32[1024]{0:T(1024)} %tgain.1, ...), custom_call_target="tpu_custom_call" | custom-call | tf_op jit(solution)/shard_map/front/pallas_call | solution.py:437
  27.2 5.0 %back.1 = (f32[32,1024]{1,0:T(8,128)}, bf16[2048,768]{1,0:T(8,128)(2,1)}) custom-call(f32[32,1024]{1,0:T(8,128)S(1)} %get-tuple-element.10.ge, f32[32,1024]{1,0:T(8,128)S(1)} %get-tuple-element.11.grad, bf16[2048,1024]{1,0:T(8,128)(2,1)S(1)} %get-tuple-element.12.h, bf16[2048,768]{1,0:T(8,128)(2,1)S(1)} %get-tuple-element.13.xs, ...), custom_call_target="tpu_custom_call" | custom-call | tf_op jit(solution)/shard_map/back/pallas_call | solution.py:493
